TPU v7x, 32 devices: a whole 2x2x4 slice. The times are simulated.
32 devices in a mesh: blk: 8 (over y, x, core), org: 4 (over z).
Axes of the slice: x: 2, y: 2, z: 4, core: 2. Of those that a mesh axis runs over, the one named last changes fastest.
Arguments:
- warm_labels: float32 [64, 512, 1024], P('blk', None, 'org'), may hold values from 0 to 6
- link_costs: float32 [4, 64, 512], P(None, 'blk'), may hold values from 0.05 to 1.5
- anchor_nodes: int32 [1024], P('org'), may hold values from 0 to 32767
- demand: float32 [1024], P('org'), may hold values from 0.2 to 2
Outputs:
- labels: float32 [64, 512, 1024], P('blk', None, 'org')
- link_weights: float32 [4, 64, 512], P(None, 'blk', 'org')
Inputs may be any that keep to these rules, and one draw needn't show every extreme that they name: `anchor_nodes`: node numbers r * 512 + c.
All inputs are finite; a program needn't handle non-finite values.
Results may differ from a plain program's by a relative error of at most 0.0003.
Values sent between devices are 32-bit elements; how exact they have to be, the bound alone decides.
A program may use at most 128 MiB of HBM per device.

v0:
```python
import functools

import jax
import jax.numpy as jnp
from jax import lax
from jax.experimental import pallas as pl
from jax.experimental.pallas import tpu as pltpu
from jax.sharding import PartitionSpec as P

INNER = 2
ROUNDS = 3
STEPS = INNER * ROUNDS
HALO = STEPS + 1

far_value = 1000000000.0
temper = 0.5
LANES = 128
PAD = 8
CHUNK = 64
MESH = pl.DeviceIdType.MESH
GROUPS = ((1, HALO - 3), (HALO - 2, HALO - 1), (HALO, HALO))


def kernel(n, m, rows, cols, halves, warm, costs, anchors, demand, out, weights, grid, wide, raw, turned, sums, share,
           landed, relay, decay, row_send, row_recv, relay_in, relay_out, cost_send, cost_recv, org_send, org_recv, local_sem, out_sem):
    me = lax.axis_index("blk")
    org = lax.axis_index("org")
    has_top = me > 0
    has_bottom = me < n - 1
    top = {"blk": jnp.maximum(me - 1, 0)}
    bottom = {"blk": jnp.minimum(me + 1, n - 1)}
    first, last = HALO, HALO + rows - 1
    inner = pl.ds(PAD, cols)
    sides = ((has_top, top), (has_bottom, bottom))
    mid = n // 2
    relayed = n == 8
    via = (0, n - 1)
    goal = (mid - 1, mid)
    splits = tuple(relayed and me == goal[1 - side] for side in range(2))
    cut = cols // 2

    barrier = pltpu.get_barrier_semaphore()
    for there, who in sides:
        @pl.when(there)
        def _():
            pl.semaphore_signal(barrier, inc=1, device_id=who, device_id_type=MESH)
    for d in range(1, m):
        pl.semaphore_signal(barrier, inc=1, device_id={"org": lax.rem(org + d, m)}, device_id_type=MESH)
    if relayed:
        for a, b in ((mid - 1, 0), (mid - 1, n - 1), (mid, 0), (mid, n - 1)):
            for mine, other in ((a, b), (b, a)):
                @pl.when(me == mine)
                def _():
                    pl.semaphore_signal(barrier, inc=1, device_id={"blk": other}, device_id_type=MESH)
    own_cost = pltpu.make_async_copy(costs, raw.at[0], local_sem.at[halves])
    own_cost.start()

    def own_rows(h):
        return pltpu.make_async_copy(
            warm.at[:, :, pl.ds(h * LANES, LANES)],
            grid.at[0, h, pl.ds(first, rows), inner, :],
            local_sem.at[h])
    for h in range(halves):
        own_rows(h).start()
    pl.semaphore_wait(barrier, m - 1 + jnp.where(has_top, 1, 0) + jnp.where(has_bottom, 1, 0)
                      + (jnp.where((me == 0) | (me == n - 1) | (me == mid) | (me == mid - 1), 2, 0) if relayed else 0))

    def cost_copy(side):
        return pltpu.make_async_remote_copy(
            src_ref=costs, dst_ref=raw.at[2 - side], send_sem=cost_send.at[side], recv_sem=cost_recv.at[side],
            device_id=sides[side][1], device_id_type=MESH)

    def ranges(side, g):
        low, high = GROUPS[g]
        count = high - low + 1
        if side == 0:
            return pl.ds(low - 1, count), pl.ds(last + low, count), pl.ds(low - 1, count)
        return pl.ds(rows - high, count), pl.ds(first - high, count), pl.ds(first - high, count)

    def lane_range(h):
        return pl.ds(pl.multiple_of(h * LANES, LANES), LANES)

    def row_copy(side, h, g, width):
        source, target, _ = ranges(side, g)
        return pltpu.make_async_remote_copy(
            src_ref=warm.at[source, pl.ds(0, width), lane_range(h)],
            dst_ref=grid.at[0, h, target, pl.ds(PAD, width), :],
            send_sem=row_send.at[side, h, g, 0], recv_sem=row_recv.at[side, h, g, 0],
            device_id=sides[side][1], device_id_type=MESH)

    def to_relay(side, h, g):
        source, _, slots = ranges(side, g)
        return pltpu.make_async_remote_copy(
            src_ref=warm.at[source, pl.ds(cut, cols - cut), lane_range(h)],
            dst_ref=relay.at[h, slots],
            send_sem=row_send.at[side, h, g, 1], recv_sem=relay_in.at[h, g],
            device_id={"blk": via[side]}, device_id_type=MESH)

    def from_relay(side, h, g):
        _, target, slots = ranges(side, g)
        return pltpu.make_async_remote_copy(
            src_ref=relay.at[h, slots],
            dst_ref=grid.at[0, h, target, pl.ds(PAD + cut, cols - cut), :],
            send_sem=relay_out.at[h, g], recv_sem=row_recv.at[side, h, g, 1],
            device_id={"blk": goal[side]}, device_id_type=MESH)

    def each_send(h, g, act):
        for side in range(2):
            there, split = sides[side][0], splits[side]
            @pl.when(there & jnp.logical_not(split) if relayed else there)
            def _():
                act(row_copy(side, h, g, cols))
            if relayed:
                @pl.when(split)
                def _():
                    act(to_relay(side, h, g))
                    act(row_copy(side, h, g, cut))

    def arrive(h, g):
        for side in range(2):
            there, split = sides[1 - side][0], splits[1 - side]
            @pl.when(there & jnp.logical_not(split) if relayed else there)
            def _():
                row_copy(side, h, g, cols).wait_recv()
            if relayed:
                @pl.when(split)
                def _():
                    row_copy(side, h, g, cut).wait_recv()
                    from_relay(side, h, g).wait_recv()

    for side in range(2):
        @pl.when(sides[side][0])
        def _():
            cost_copy(side).start()
    for h in range(halves):
        for g in range(len(GROUPS)):
            each_send(h, g, lambda copy: copy.start())

    edge = jnp.full((PAD, LANES), far_value, jnp.float32)
    total = rows + 2 * HALO

    def fill_edges(r, carry):
        for b in range(2):
            for h in range(halves):
                grid[b, h, r, pl.ds(0, PAD), :] = edge
                grid[b, h, r, pl.ds(PAD + cols, PAD), :] = edge
        return carry
    lax.fori_loop(0, total, fill_edges, 0)
    raw[3] = jnp.zeros_like(raw[3])
    for missing, block, begin in ((me == 0, 1, 0), (me == n - 1, 2, last + 1)):
        @pl.when(missing)
        def _():
            raw[block] = jnp.full(raw.shape[1:], far_value, jnp.float32)
            def fill(r, carry):
                for h in range(halves):
                    grid[0, h, begin + r, inner, :] = jnp.full((cols, LANES), far_value, jnp.float32)
                return carry
            lax.fori_loop(0, HALO, fill, 0)

    own_cost.wait()
    for side in range(2):
        @pl.when(sides[1 - side][0])
        def _():
            cost_copy(side).wait_recv()
    turned[...] = jnp.transpose(raw[...].reshape(4 * 4 * rows, cols))

    def widen(i, carry):
        piece = turned[pl.ds(pl.multiple_of(i * 8, 8), 8), :]
        for r in range(1, total - 1):
            if r < first:
                block, row = 1, rows - first + r
            elif r <= last:
                block, row = 0, r - first
            else:
                block, row = 2, r - last - 1
            for k in range(4):
                lane = (block * 4 + k) * rows + row
                wide[k, r, pl.ds(pl.multiple_of(i * 8, 8), 8), :] = jnp.broadcast_to(piece[:, lane:lane + 1], (8, LANES))
        return carry
    lax.fori_loop(0, cols // 8, widen, 0)

    def place(h, r):
        names = anchors[h]
        base = (me * rows + r - first) * cols
        for i in range(cols // CHUNK):
            node = lax.broadcasted_iota(jnp.int32, (CHUNK, LANES), 0) + (base + i * CHUNK)
            at = pl.ds(PAD + i * CHUNK, CHUNK)
            grid[0, h, r, at, :] = jnp.where(node == names, 0.0, grid[0, h, r, at, :])

    def relax(h, r, s):
        old, new = lax.rem(s + 1, 2), lax.rem(s, 2)
        for i in range(cols // CHUNK):
            c0 = PAD + i * CHUNK
            at, cut = pl.ds(c0, CHUNK), pl.ds(i * CHUNK, CHUNK)
            best = grid[old, h, r, at, :]
            best = jnp.minimum(best, grid[old, h, r, pl.ds(c0 - 1, CHUNK), :] + wide[0, r, cut, :])
            best = jnp.minimum(best, grid[old, h, r, pl.ds(c0 + 1, CHUNK), :] + wide[1, r, cut, :])
            best = jnp.minimum(best, grid[old, h, r - 1, at, :] + wide[2, r, cut, :])
            best = jnp.minimum(best, grid[old, h, r + 1, at, :] + wide[3, r, cut, :])
            grid[new, h, r, at, :] = best

    ones = jnp.ones((8, 2 * LANES), jnp.bfloat16)
    sums[...] = jnp.zeros_like(sums)
    middle = rows // 2
    zero_edge = jnp.zeros((PAD, LANES), jnp.float32)
    for r in range(rows + 2):
        decay[r, pl.ds(0, PAD), :] = zero_edge
        decay[r, pl.ds(PAD + cols, PAD), :] = zero_edge

    def begin(h, carry):
        own_rows(h).wait()

        def place_own(r, carry):
            place(h, r)
            return carry
        lax.fori_loop(first, last + 1, place_own, 0)
        for s in range(1, middle):
            def inside(r, carry):
                relax(h, r, jnp.int32(s))
                return carry
            lax.fori_loop(first + s, last - s + 1, inside, 0)
        return carry
    lax.fori_loop(0, halves, begin, 0)

    def half(h, carry):
        if relayed:
            for side in range(2):
                @pl.when(me == via[side])
                def _():
                    for g in range(len(GROUPS)):
                        to_relay(side, h, g).wait_recv()
                        from_relay(side, h, g).start()

        def stage(j, carry):
            place(h, first - j)
            place(h, last + j)

            def diagonal(s, carry):
                relax(h, first - j + s, s)
                relax(h, last + j - s, s)
                return carry
            return lax.fori_loop(1, jnp.minimum(STEPS, j + middle - 1) + 1, diagonal, carry)

        def small(r, carry):
            for i in range(cols // CHUNK):
                at = pl.ds(PAD + i * CHUNK, CHUNK)
                decay[r - first + 1, at, :] = jnp.exp(-temper * grid[0, h, r, at, :])
            return carry

        def add_link(k, own, r, row, start):
            term = own * decay[row - first + 1, pl.ds(start, cols), :]
            high = term.astype(jnp.bfloat16)
            low = (term - high.astype(jnp.float32)).astype(jnp.bfloat16)
            part = lax.dot_general(ones, jnp.concatenate([high, low], axis=1), (((1,), (1,)), ((), ())),
                                   preferred_element_type=jnp.float32)
            sums[k, pl.ds(r - first, 1), :] += part[0:1]

        def growth(r):
            return demand[h] * jnp.exp(temper * grid[0, h, r, inner, :])

        def along(r, carry):
            own = growth(r)
            add_link(0, own, r, r, PAD - 1)
            add_link(1, own, r, r, PAD + 1)
            return carry

        def across(r, carry):
            add_link(3, growth(r), r, r + 1, PAD)
            add_link(2, growth(r + 1), r + 1, r, PAD)
            return carry

        for g in range(len(GROUPS) - 1):
            arrive(h, g)
            lax.fori_loop(GROUPS[g][0], GROUPS[g][1] + 1, stage, 0)
        out_copy(h).start()
        lax.fori_loop(first, last + 1, small, 0)
        lax.fori_loop(first, last + 1, along, 0)
        lax.fori_loop(first, last, across, 0)
        g = len(GROUPS) - 1
        arrive(h, g)
        lax.fori_loop(GROUPS[g][0], GROUPS[g][1] + 1, stage, 0)
        for r, k, row in ((first, 2, first - 1), (last, 3, last + 1)):
            small(row, 0)
            add_link(k, growth(r), r, row, PAD)
        return carry

    def out_copy(h):
        lanes = pl.ds(pl.multiple_of(h * LANES, LANES), LANES)
        return pltpu.make_async_copy(grid.at[0, h, pl.ds(first, rows), inner, :], out.at[:, :, lanes], out_sem.at[h])

    lax.fori_loop(0, halves, half, 0)

    scale = 1.0 / (m * halves * LANES)
    ours = sums[...] * jnp.exp(-temper * raw[0]) * scale
    width = cols // m
    for p in range(m):
        share[p] = ours[:, :, p * width:(p + 1) * width]

    def org_copy(d):
        peer = lax.rem(org + d, m)
        return pltpu.make_async_remote_copy(
            src_ref=share.at[peer], dst_ref=landed.at[d - 1], send_sem=org_send.at[d - 1], recv_sem=org_recv.at[d - 1],
            device_id={"org": peer}, device_id_type=MESH)
    for d in range(1, m):
        org_copy(d).start()
    final = share[org]
    for d in range(1, m):
        org_copy(d).wait_recv()
        final += landed[d - 1]
    weights[...] = final

    for d in range(1, m):
        org_copy(d).wait_send()
    for h in range(halves):
        out_copy(h).wait()
    for side in range(2):
        @pl.when(sides[side][0])
        def _():
            cost_copy(side).wait_send()
    for h in range(halves):
        for g in range(len(GROUPS)):
            each_send(h, g, lambda copy: copy.wait_send())
            if relayed:
                for side in range(2):
                    @pl.when(me == via[side])
                    def _():
                        from_relay(side, h, g).wait_send()


def local(n, m, warm_labels, link_costs, anchor_nodes, demand):
    rows, cols, count = warm_labels.shape
    halves = count // LANES
    total = rows + 2 * HALO
    width = cols // m
    any_space = pl.BlockSpec(memory_space=pl.ANY)
    vmem = pl.BlockSpec(memory_space=pltpu.VMEM)
    dma = pltpu.SemaphoreType.DMA
    return pl.pallas_call(
        functools.partial(kernel, n, m, rows, cols, halves),
        out_shape=(
            jax.ShapeDtypeStruct((rows, cols, count), jnp.float32),
            jax.ShapeDtypeStruct((4, rows, width), jnp.float32),
        ),
        in_specs=[any_space, any_space, vmem, vmem],
        out_specs=(any_space, vmem),
        scratch_shapes=[
            pltpu.VMEM((2, halves, total, cols + 2 * PAD, LANES), jnp.float32),
            pltpu.VMEM((4, total, cols, LANES), jnp.float32),
            pltpu.VMEM((4, 4, rows, cols), jnp.float32),
            pltpu.VMEM((cols, 16 * rows), jnp.float32),
            pltpu.VMEM((4, rows, cols), jnp.float32),
            pltpu.VMEM((m, 4, rows, width), jnp.float32),
            pltpu.VMEM((max(m - 1, 1), 4, rows, width), jnp.float32),
            pltpu.VMEM((halves, HALO, cols - cols // 2, LANES), jnp.float32),
            pltpu.VMEM((rows + 2, cols + 2 * PAD, LANES), jnp.float32),
            dma((2, halves, len(GROUPS), 2)),
            dma((2, halves, len(GROUPS), 2)),
            dma((halves, len(GROUPS))),
            dma((halves, len(GROUPS))),
            dma((2,)),
            dma((2,)),
            dma((max(m - 1, 1),)),
            dma((max(m - 1, 1),)),
            dma((halves + 1,)),
            dma((halves,)),
        ],
        compiler_params=pltpu.CompilerParams(collective_id=0, has_side_effects=True, vmem_limit_bytes=60 * 1024 * 1024),
    )(warm_labels, link_costs, anchor_nodes.reshape(halves, 1, LANES), demand.reshape(halves, 1, LANES))


def solution(mesh):
    placed = (P("blk", None, "org"), P(None, "blk", None), P("org"), P("org"))
    return jax.shard_map(
        functools.partial(local, mesh.shape["blk"], mesh.shape["org"]),
        mesh=mesh,
        in_specs=placed,
        out_specs=(P("blk", None, "org"), P(None, "blk", "org")),
        check_vma=False,
    )
```

profile of v0, /device:TPU:1, one launch (start us, length us, event | category | flops | bytes accessed | tf_op | source)
XLA Modules:
  0.0 83.7 jit_solution(3159955196474723322)
XLA Ops:
  0.6 77.9 %shard_map.59 = (f32[8,512,256]{2,1,0:T(8,128)}, f32[4,8,128]{2,1,0:T(8,128)}) custom-call(f32[8,512,256]{2,1,0:T(8,128)} %warm.1, f32[4,8,512]{2,1,0:T(8,128)} %costs.1, s32[2,1,128]{2,1,0:T(1,128)} %bitcast.2, f32[2,1,128]{2,1,0:T(1,128)} %bitcast.3), custom_call_target="tpu_custom_call" | custom-call | tf_op jit(solution)/shard_map/pallas_call | solution.py:338
  78.5 0.0 copy-start
  78.6 4.5 %copy.8 = f32[8,512,256]{2,1,0:T(8,128)} copy(f32[8,512,256]{2,1,0:T(8,128)} %get-tuple-element.4) | data formatting | bytes 8388608
  83.1 0.0 copy-done
  83.1 0.6 copy.9
Async XLA Ops:
  78.5 4.5 %copy-start = (f32[4,8,128]{2,1,0:T(8,128)S(1)}, f32[4,8,128]{2,1,0:T(8,128)}, u32[]{:S(2)}) copy-start(f32[4,8,128]{2,1,0:T(8,128)} %get-tuple-element.5) | copy-start | bytes 49156
where the time goes:
time: 83.8 us; the launch traced here: 83.7 us
  Pallas kernels  77.9 us (93%)
  local copies, waits for them, and re-layouts  5.11 us (6%)
    pallas_call x1, Pallas kernels, local(): pl.pallas_call(functools.partial(kernel, n, m, rows, cols, halves), out_s...  77.9 us
    unnamed x4, local copies, waits for them, and re-layouts  5.11 us

commit v1 on v0

v1 whole, which is shorter than its diff:
```python
import functools
import math

import jax
import jax.numpy as jnp
from jax import lax
from jax.experimental import pallas as pl
from jax.experimental.pallas import tpu as pltpu
from jax.sharding import PartitionSpec as P

INNER = 2
ROUNDS = 3
STEPS = INNER * ROUNDS
HALO = STEPS + 1

far_value = 1000000000.0
temper = 0.5
RATE = temper * math.log2(math.e)
LANES = 128
PAD = 8
CHUNK = 32
BAND = 64
SPAN = 256
MESH = pl.DeviceIdType.MESH


def kernel(n, m, rows, cols, halves, warm, costs, anchors, demand, final, weights, grid, wide, raw, turned, decay, growth, tail,
           relay, sums, share, landed, near_out, near_in, row_send, row_recv, relay_in, relay_out, cost_send, cost_recv,
           org_send, org_recv, near_send, near_recv, local_sem):
    me = lax.axis_index("blk")
    org = lax.axis_index("org")
    has_top = me > 0
    has_bottom = me < n - 1
    top = jnp.maximum(me - 1, 0)
    bottom = jnp.minimum(me + 1, n - 1)
    first, last = HALO, HALO + rows - 1
    total = rows + 2 * HALO
    inner = pl.ds(PAD, cols)
    sides = ((has_top, top), (has_bottom, bottom))
    mid = n // 2
    relayed = n == 8
    via = (0, n - 1)
    goal = (mid - 1, mid)
    splits = tuple(relayed and me == goal[1 - side] for side in range(2))
    cut = cols // 2
    width = cols // m
    late = lax.rem(me, 2)
    early = 1 - late
    last_unit = STEPS * halves

    barrier = pltpu.get_barrier_semaphore()
    for there, who in sides:
        @pl.when(there)
        def _():
            for p in range(m):
                pl.semaphore_signal(barrier, inc=1, device_id={"blk": who, "org": p}, device_id_type=MESH)
    for d in range(1, m):
        pl.semaphore_signal(barrier, inc=1, device_id={"org": lax.rem(org + d, m)}, device_id_type=MESH)
    if relayed:
        for a, b in ((mid - 1, 0), (mid - 1, n - 1), (mid, 0), (mid, n - 1)):
            for mine, other in ((a, b), (b, a)):
                @pl.when(me == mine)
                def _():
                    pl.semaphore_signal(barrier, inc=1, device_id={"blk": other}, device_id_type=MESH)
    own_cost = pltpu.make_async_copy(costs, raw.at[0], local_sem.at[halves])
    own_cost.start()

    def own_rows(h):
        return pltpu.make_async_copy(
            warm.at[:, :, pl.ds(h * LANES, LANES)],
            grid.at[0, h, pl.ds(first, rows), inner, :],
            local_sem.at[h])
    for h in range(halves):
        own_rows(h).start()
    pl.semaphore_wait(barrier, m - 1 + jnp.where(has_top, m, 0) + jnp.where(has_bottom, m, 0)
                      + (jnp.where((me == 0) | (me == n - 1) | (me == mid) | (me == mid - 1), 2, 0) if relayed else 0))

    def cost_copy(side):
        return pltpu.make_async_remote_copy(
            src_ref=costs, dst_ref=raw.at[2 - side], send_sem=cost_send.at[side], recv_sem=cost_recv.at[side],
            device_id={"blk": sides[side][1]}, device_id_type=MESH)

    def source(side, j, h, start, count):
        row = jnp.where(side == 0, j - 1, rows - j)
        return warm.at[row, pl.ds(start, count), pl.ds(h * LANES, LANES)]

    def target(side, j, h, start, count):
        if isinstance(j, int) and j == HALO:
            return tail.at[1 - side, pl.ds(start, count), :]
        row = jnp.where(side == 0, last + j, first - j)
        return grid.at[0, h, row, pl.ds(PAD + start, count), :]

    def unit(j, h):
        return last_unit if isinstance(j, int) and j == HALO else (j - 1) * halves + h

    def row_copy(side, j, h, count):
        u = unit(j, h)
        return pltpu.make_async_remote_copy(
            src_ref=source(side, j, h, 0, count), dst_ref=target(side, j, h, 0, count),
            send_sem=row_send.at[side, u, 0], recv_sem=row_recv.at[side, u, 0],
            device_id={"blk": jnp.where(side == 0, top, bottom)}, device_id_type=MESH)

    def to_relay(side, j, h):
        u = unit(j, h)
        return pltpu.make_async_remote_copy(
            src_ref=source(side, j, h, cut, cols - cut), dst_ref=relay.at[u],
            send_sem=row_send.at[side, u, 1], recv_sem=relay_in.at[u],
            device_id={"blk": via[side]}, device_id_type=MESH)

    def from_relay(side, j, h):
        u = unit(j, h)
        return pltpu.make_async_remote_copy(
            src_ref=relay.at[u], dst_ref=target(side, j, h, cut, cols - cut),
            send_sem=relay_out.at[u], recv_sem=row_recv.at[side, u, 1],
            device_id={"blk": goal[side]}, device_id_type=MESH)

    def each_send(j, h, side, act):
        there, split = sides[side][0], splits[side]
        @pl.when(there & jnp.logical_not(split) if relayed else there)
        def _():
            act(row_copy(side, j, h, cols))
        if relayed:
            @pl.when(split)
            def _():
                act(to_relay(side, j, h))
                act(row_copy(side, j, h, cut))

    def all_sends(act):
        def body(j, carry):
            for h in range(halves):
                for side in range(2):
                    each_send(j, h, side, act)
            return carry
        lax.fori_loop(1, STEPS + 1, body, 0)
        for side in range(2):
            each_send(HALO, 1 - side, side, act)

    def arrive(halo, j, h):
        side = 1 - halo
        there = jnp.where(halo == 0, has_top, has_bottom)
        split = jnp.where(halo == 0, me == goal[1], me == goal[0]) & there
        @pl.when(there & jnp.logical_not(split) if relayed else there)
        def _():
            pltpu.make_async_remote_copy(
                src_ref=source(0, 1, 0, 0, cols), dst_ref=target(side, j, h, 0, cols),
                send_sem=row_send.at[side, unit(j, h), 0], recv_sem=row_recv.at[side, unit(j, h), 0],
                device_id={"blk": bottom}, device_id_type=MESH).wait_recv()
        if relayed:
            @pl.when(split)
            def _():
                for part, start, count in ((0, 0, cut), (1, cut, cols - cut)):
                    pltpu.make_async_remote_copy(
                        src_ref=source(0, 1, 0, start, count), dst_ref=target(side, j, h, start, count),
                        send_sem=row_send.at[side, unit(j, h), part], recv_sem=row_recv.at[side, unit(j, h), part],
                        device_id={"blk": bottom}, device_id_type=MESH).wait_recv()

    def forward(j, h):
        if relayed:
            for side in range(2):
                @pl.when(me == via[side])
                def _():
                    k = 1 - side if h is None else h
                    to_relay(side, j, k).wait_recv()
                    from_relay(side, j, k).start()

    for side in range(2):
        @pl.when(sides[side][0])
        def _():
            cost_copy(side).start()
    all_sends(lambda copy: copy.start())

    edge = jnp.full((PAD, LANES), far_value, jnp.float32)
    zero_edge = jnp.zeros((PAD, LANES), jnp.float32)

    def fill_edges(r, carry):
        for b in range(2):
            for h in range(halves):
                grid[b, h, r, pl.ds(0, PAD), :] = edge
                grid[b, h, r, pl.ds(PAD + cols, PAD), :] = edge
        return carry
    lax.fori_loop(0, total, fill_edges, 0)

    def fill_decay(r, carry):
        for h in range(halves):
            decay[h, r, pl.ds(0, PAD), :] = zero_edge
            decay[h, r, pl.ds(PAD + cols, PAD), :] = zero_edge
        return carry
    lax.fori_loop(0, rows + 2, fill_decay, 0)
    sums[...] = jnp.zeros_like(sums)
    raw[3] = jnp.zeros_like(raw[3])

    def fill_row(r):
        for h in range(halves):
            grid[0, h, r, inner, :] = jnp.full((cols, LANES), far_value, jnp.float32)
    fill_row(0)
    fill_row(total - 1)
    for missing, block, begin in ((me == 0, 1, 1), (me == n - 1, 2, last + 1)):
        @pl.when(missing)
        def _():
            raw[block] = jnp.full(raw.shape[1:], far_value, jnp.float32)
            def fill(r, carry):
                fill_row(begin + r)
                return carry
            lax.fori_loop(0, STEPS, fill, 0)

    def place(r):
        base = (me * rows + r - first) * cols
        names = [anchors[h] for h in range(halves)]
        for i in range(cols // CHUNK):
            node = lax.broadcasted_iota(jnp.int32, (CHUNK, LANES), 0) + (base + i * CHUNK)
            at = pl.ds(PAD + i * CHUNK, CHUNK)
            for h in range(halves):
                grid[0, h, r, at, :] = jnp.where(node == names[h], 0.0, grid[0, h, r, at, :])

    for h in range(halves):
        own_rows(h).wait()

    def place_own(r, carry):
        place(r)
        return carry
    lax.fori_loop(first, last + 1, place_own, 0)

    own_cost.wait()
    for side in range(2):
        @pl.when(sides[1 - side][0])
        def _():
            cost_copy(side).wait_recv()
    turned[...] = jnp.transpose(raw[...].reshape(4 * 4 * rows, cols))

    def widen(i, carry):
        at = pl.ds(pl.multiple_of(i * BAND, BAND), BAND)
        piece = turned[at, :]
        for r in range(1, total - 1):
            if r < first:
                block, row = 1, rows - first + r
            elif r <= last:
                block, row = 0, r - first
            else:
                block, row = 2, r - last - 1
            for k in range(4):
                lane = (block * 4 + k) * rows + row
                wide[k, r - 1, at, :] = jnp.broadcast_to(piece[:, lane:lane + 1], (BAND, LANES))
        return carry
    lax.fori_loop(0, cols // BAND, widen, 0)

    def best_of(old, r, i, hs):
        c0 = PAD + i * CHUNK
        at, mine = pl.ds(c0, CHUNK), pl.ds(i * CHUNK, CHUNK)
        price = [wide[k, r - 1, mine, :] for k in range(4)]
        result = []
        for h in hs:
            best = grid[old, h, r, at, :]
            best = jnp.minimum(best, grid[old, h, r, pl.ds(c0 - 1, CHUNK), :] + price[0])
            best = jnp.minimum(best, grid[old, h, r, pl.ds(c0 + 1, CHUNK), :] + price[1])
            best = jnp.minimum(best, grid[old, h, r - 1, at, :] + price[2])
            best = jnp.minimum(best, grid[old, h, r + 1, at, :] + price[3])
            result.append(best)
        return at, mine, result

    def relax(r, s, hs):
        old, new = lax.rem(s + 1, 2), lax.rem(s, 2)
        for i in range(cols // CHUNK):
            at, _, result = best_of(old, r, i, hs)
            for h, best in zip(hs, result):
                grid[new, h, r, at, :] = best

    both = tuple(range(halves))

    def finish(halo, j):
        r = jnp.where(halo == 0, first - j + STEPS, last + j - STEPS)
        q = r - first
        wants = [demand[h] for h in both]
        for i in range(cols // CHUNK):
            at, mine, result = best_of((STEPS + 1) % 2, r, i, both)
            for h, best in zip(both, result):
                final[q, mine, pl.ds(h * LANES, LANES)] = best
                power = best * RATE
                decay[h, q + 1, at, :] = jnp.exp2(-power)
                growth[h, q + 1, mine, :] = wants[h] * jnp.exp2(power)

    middle = rows // 2
    for s in range(1, middle):
        def inside(r, carry):
            relax(r, jnp.int32(s), both)
            return carry
        lax.fori_loop(first + s, last - s + 1, inside, 0)

    def stage(halo, j):
        for h in both:
            arrive(halo, j, h)
        place(jnp.where(halo == 0, first - j, last + j))

        def diagonal(s, carry):
            relax(jnp.where(halo == 0, first - j + s, last + j - s), s, both)
            return carry
        lax.fori_loop(1, jnp.minimum(STEPS - 1, j + middle - 1) + 1, diagonal, 0)

    def pair(q):
        return jnp.where(q == 0, early, late)

    def opening(j, carry):
        for h in both:
            forward(j, h)

        def one(q, carry):
            stage(pair(q), j)
            return carry
        return lax.fori_loop(0, 2, one, carry)

    def closing(j, carry):
        for h in both:
            forward(j, h)

        def one(q, carry):
            stage(pair(q), j)
            finish(pair(q), j)
            return carry
        return lax.fori_loop(0, 2, one, carry)

    ones = jnp.ones((8, 2 * LANES), jnp.bfloat16)

    def link(own, other, shift, hs, store):
        for c in range(0, cols, SPAN):
            term = None
            for h in hs:
                piece = growth[h, own, pl.ds(c, SPAN), :] * decay[h, other, pl.ds(PAD + c + shift, SPAN), :]
                term = piece if term is None else term + piece
            high = term.astype(jnp.bfloat16)
            low = (term - high.astype(jnp.float32)).astype(jnp.bfloat16)
            part = lax.dot_general(ones, jnp.concatenate([high, low], axis=1), (((1,), (1,)), ((), ())),
                                   preferred_element_type=jnp.float32)
            store(pl.ds(c, SPAN), part[0:1])

    def add_link(k, r, row, shift, hs):
        def store(at, part):
            sums[k, pl.ds(r - first, 1), at] = part
        link(r - first + 1, row - first + 1, shift, hs, store)

    def along(r, carry):
        add_link(0, r, r, -1, both)
        add_link(1, r, r, 1, both)
        return carry

    def across(r, carry):
        add_link(3, r, r + 1, 0, both)
        add_link(2, r + 1, r, 0, both)
        return carry

    def outer(halo):
        r0 = jnp.where(halo == 0, first - HALO, last + HALO)
        step = jnp.where(halo == 0, 1, -1)

        def diagonal(s, carry):
            relax(r0 + step * s, s, (halo,))
            return carry
        lax.fori_loop(1, STEPS + 1, diagonal, 0)

    scale = 1.0 / (m * halves * LANES)

    def cross(halo):
        there = jnp.where(halo == 0, has_top, has_bottom)
        r0 = jnp.where(halo == 0, first - HALO, last + HALO)
        step = jnp.where(halo == 0, 1, -1)
        own = jnp.where(halo == 0, 1, rows)
        other = jnp.where(halo == 0, 0, rows + 1)
        arrive(halo, HALO, halo)

        @pl.when(there)
        def _():
            base = (me * rows + r0 - first) * cols
            names, wants = anchors[halo], demand[halo]
            for i in range(cols // CHUNK):
                at, mine = pl.ds(PAD + i * CHUNK, CHUNK), pl.ds(i * CHUNK, CHUNK)
                node = lax.broadcasted_iota(jnp.int32, (CHUNK, LANES), 0) + (base + i * CHUNK)
                value = jnp.where(node == names, 0.0, tail[halo, mine, :])
                for t in range(1, STEPS + 1):
                    value = value + wide[2 + halo, r0 + step * t - 1, mine, :]
                power = jnp.minimum(value, grid[STEPS % 2, halo, r0 + step * STEPS, at, :]) * RATE
                decay[halo, other, at, :] = jnp.exp2(-power)
                growth[halo, other, mine, :] = wants * jnp.exp2(power)

            def mine_store(at, part):
                sums[2 + halo, pl.ds(own - 1, 1), at] = part
            link(own, other, 0, (halo,), mine_store)

            def near_store(at, part):
                fee = raw[1 + halo, 3 - halo, pl.ds(jnp.where(halo == 0, rows - 1, 0), 1), at]
                value = part * jnp.exp(-temper * fee) * scale
                for c in range(0, at.size, width):
                    near_out[halo, (at.start + c) // width] = value[:, c:c + width]
            link(other, own, 0, (halo,), near_store)

    def near_copy(halo, p):
        return pltpu.make_async_remote_copy(
            src_ref=near_out.at[halo, p], dst_ref=near_in.at[1 - halo, org], send_sem=near_send.at[halo, p],
            recv_sem=near_recv.at[1 - halo, org], device_id={"blk": sides[halo][1], "org": p}, device_id_type=MESH)

    def near_wait(halo, p):
        pltpu.make_async_remote_copy(
            src_ref=near_out.at[halo, p], dst_ref=near_in.at[halo, p], send_sem=near_send.at[halo, p],
            recv_sem=near_recv.at[halo, p], device_id={"blk": sides[halo][1], "org": p}, device_id_type=MESH).wait_recv()

    lax.fori_loop(1, 3, opening, 0)
    lax.fori_loop(3, STEPS, closing, 0)
    for h in both:
        forward(STEPS, h)
    forward(HALO, None)

    def closing_side(q, carry):
        halo = pair(q)
        stage(halo, STEPS)
        finish(halo, STEPS)
        outer(halo)
        low = jnp.where(q == 0, jnp.where(late == 0, first + 1, first), jnp.where(late == 0, first, last))
        high = jnp.where(q == 0, jnp.where(late == 0, last, last - 1), jnp.where(late == 0, first, last))
        lax.fori_loop(low, high + 1, along, 0)
        low = jnp.where(q == 0, jnp.where(late == 0, first + 1, first), jnp.where(late == 0, first, last - 1))
        high = jnp.where(q == 0, jnp.where(late == 0, last - 1, last - 2), jnp.where(late == 0, first, last - 1))
        lax.fori_loop(low, high + 1, across, 0)
        cross(halo)
        return carry
    lax.fori_loop(0, 2, closing_side, 0)

    ours = sums[...] * jnp.exp(-temper * raw[0]) * scale
    for p in range(m):
        share[p] = ours[:, :, p * width:(p + 1) * width]

    def org_copy(d):
        peer = lax.rem(org + d, m)
        return pltpu.make_async_remote_copy(
            src_ref=share.at[peer], dst_ref=landed.at[d - 1], send_sem=org_send.at[d - 1], recv_sem=org_recv.at[d - 1],
            device_id={"org": peer}, device_id_type=MESH)
    for halo in range(2):
        @pl.when(sides[halo][0])
        def _():
            for p in range(m):
                near_copy(halo, p).start()
    for d in range(1, m):
        org_copy(d).start()
    result = share[org]
    for d in range(1, m):
        org_copy(d).wait_recv()
        result += landed[d - 1]
    weights[...] = result
    for halo in range(2):
        @pl.when(sides[halo][0])
        def _():
            at = 0 if halo == 0 else rows - 1
            extra = weights[2 + halo, pl.ds(at, 1), :]
            for p in range(m):
                near_wait(halo, p)
                extra += near_in[halo, p]
            weights[2 + halo, pl.ds(at, 1), :] = extra

    for d in range(1, m):
        org_copy(d).wait_send()
    for side in range(2):
        @pl.when(sides[side][0])
        def _():
            cost_copy(side).wait_send()
            for p in range(m):
                near_copy(side, p).wait_send()
    all_sends(lambda copy: copy.wait_send())
    if relayed:
        for side in range(2):
            @pl.when(me == via[side])
            def _():
                def body(j, carry):
                    for h in both:
                        from_relay(side, j, h).wait_send()
                    return carry
                lax.fori_loop(1, STEPS + 1, body, 0)
                from_relay(side, HALO, 1 - side).wait_send()


def leave(rows, labels, weights, labels_out, weights_out, sems):
    copies = [pltpu.make_async_copy(labels.at[r], labels_out.at[r], sems.at[r]) for r in range(rows)]
    copies.append(pltpu.make_async_copy(weights, weights_out, sems.at[rows]))
    for copy in copies:
        copy.start()
    for copy in copies:
        copy.wait()


def local(n, m, warm_labels, link_costs, anchor_nodes, demand):
    rows, cols, count = warm_labels.shape
    halves = count // LANES
    total = rows + 2 * HALO
    width = cols // m
    units = STEPS * halves + 1
    any_space = pl.BlockSpec(memory_space=pl.ANY)
    vmem = pl.BlockSpec(memory_space=pltpu.VMEM)
    dma = pltpu.SemaphoreType.DMA
    labels, weights = pl.pallas_call(
        functools.partial(kernel, n, m, rows, cols, halves),
        out_shape=(
            pltpu.VMEM((rows, cols, count), jnp.float32),
            pltpu.VMEM((4, rows, width), jnp.float32),
        ),
        in_specs=[any_space, any_space, vmem, vmem],
        out_specs=(vmem, vmem),
        scratch_shapes=[
            pltpu.VMEM((2, halves, total, cols + 2 * PAD, LANES), jnp.float32),
            pltpu.VMEM((4, total - 2, cols, LANES), jnp.float32),
            pltpu.VMEM((4, 4, rows, cols), jnp.float32),
            pltpu.VMEM((cols, 16 * rows), jnp.float32),
            pltpu.VMEM((halves, rows + 2, cols + 2 * PAD, LANES), jnp.float32),
            pltpu.VMEM((halves, rows + 2, cols, LANES), jnp.float32),
            pltpu.VMEM((2, cols, LANES), jnp.float32),
            pltpu.VMEM((units, cols - cols // 2, LANES), jnp.float32),
            pltpu.VMEM((4, rows, cols), jnp.float32),
            pltpu.VMEM((m, 4, rows, width), jnp.float32),
            pltpu.VMEM((max(m - 1, 1), 4, rows, width), jnp.float32),
            pltpu.VMEM((2, m, 1, width), jnp.float32),
            pltpu.VMEM((2, m, 1, width), jnp.float32),
            dma((2, units, 2)),
            dma((2, units, 2)),
            dma((units,)),
            dma((units,)),
            dma((2,)),
            dma((2,)),
            dma((max(m - 1, 1),)),
            dma((max(m - 1, 1),)),
            dma((2, m)),
            dma((2, m)),
            dma((halves + 1,)),
        ],
        compiler_params=pltpu.CompilerParams(collective_id=0, has_side_effects=True, vmem_limit_bytes=58 * 1024 * 1024),
    )(warm_labels, link_costs, anchor_nodes.reshape(halves, 1, LANES), demand.reshape(halves, 1, LANES))
    labels = pltpu.with_memory_space_constraint(labels, pltpu.VMEM)
    weights = pltpu.with_memory_space_constraint(weights, pltpu.VMEM)
    return pl.pallas_call(
        functools.partial(leave, rows),
        out_shape=(
            jax.ShapeDtypeStruct((rows, cols, count), jnp.float32),
            jax.ShapeDtypeStruct((4, rows, width), jnp.float32),
        ),
        in_specs=[vmem, vmem],
        out_specs=(any_space, any_space),
        scratch_shapes=[dma((rows + 1,))],
        compiler_params=pltpu.CompilerParams(vmem_limit_bytes=8 * 1024 * 1024),
    )(labels, weights)


def solution(mesh):
    placed = (P("blk", None, "org"), P(None, "blk", None), P("org"), P("org"))
    return jax.shard_map(
        functools.partial(local, mesh.shape["blk"], mesh.shape["org"]),
        mesh=mesh,
        in_specs=placed,
        out_specs=(P("blk", None, "org"), P(None, "blk", "org")),
        check_vma=False,
    )
```

time: 83.8 us -> 73.3 us (0.87)
  Pallas kernels: 77.9 us -> 72.2 us
  local copies, waits for them, and re-layouts: 5.11 us -> 0 us
    pallas_call x1, Pallas kernels: 77.9 us -> 70.2 us  [local(): pl.pallas_call(functools.partial(kernel, n, m, rows, cols, halves), out_s...]
    unnamed x4 -> x0, local copies, waits for them, and re-layouts: 5.11 us -> none
    pallas_call x0 -> x1, Pallas kernels: none -> 2.08 us  [local(): pl.pallas_call(functools.partial(leave, rows), out_shape=(jax.ShapeDtypeS...]
where the time goes in v1:
time: 73.3 us; the launch traced here: 72.9 us
  Pallas kernels  72.2 us (98%)
    pallas_call x1, Pallas kernels, local(): pl.pallas_call(functools.partial(kernel, n, m, rows, cols, halves), out_s...  70.2 us
    pallas_call x1, Pallas kernels, local(): pl.pallas_call(functools.partial(leave, rows), out_shape=(jax.ShapeDtypeS...  2.08 us

profile of v1, /device:TPU:1, one launch (start us, length us, event | category | flops | bytes accessed | tf_op | source)
XLA Modules:
  0.0 72.9 jit_solution(3570959683906068538)
XLA Ops:
  0.6 70.2 %shard_map.59 = (f32[8,512,256]{2,1,0:T(8,128)S(1)}, f32[4,8,128]{2,1,0:T(8,128)S(1)}) custom-call(f32[8,512,256]{2,1,0:T(8,128)} %warm.1, f32[4,8,512]{2,1,0:T(8,128)} %costs.1, s32[2,1,128]{2,1,0:T(1,128)} %bitcast.2, f32[2,1,128]{2,1,0:T(1,128)} %bitcast.3), custom_call_target="tpu_custom_call" | custom-call | tf_op jit(solution)/shard_map/pallas_call | solution.py:494
  70.8 2.1 %shard_map.60 = (f32[8,512,256]{2,1,0:T(8,128)}, f32[4,8,128]{2,1,0:T(8,128)}) custom-call(f32[8,512,256]{2,1,0:T(8,128)S(1)} %get-tuple-element.4.labels, f32[4,8,128]{2,1,0:T(8,128)S(1)} %get-tuple-element.5.weights), custom_call_target="tpu_custom_call" | custom-call | tf_op jit(solution)/shard_map/pallas_call | solution.py:532

commit v2 on v1

--- a/solution.py
+++ b/solution.py
@@ -75,18 +75,26 @@
     pl.semaphore_wait(barrier, m - 1 + jnp.where(has_top, m, 0) + jnp.where(has_bottom, m, 0)
                       + (jnp.where((me == 0) | (me == n - 1) | (me == mid) | (me == mid - 1), 2, 0) if relayed else 0))
 
+    part = 4 // m
+    piece_of = pl.ds(org * part, part)
+
     def cost_copy(side):
         return pltpu.make_async_remote_copy(
-            src_ref=costs, dst_ref=raw.at[2 - side], send_sem=cost_send.at[side], recv_sem=cost_recv.at[side],
-            device_id={"blk": sides[side][1]}, device_id_type=MESH)
+            src_ref=costs.at[piece_of], dst_ref=raw.at[2 - side, piece_of], send_sem=cost_send.at[side, 0],
+            recv_sem=cost_recv.at[side, 0], device_id={"blk": sides[side][1]}, device_id_type=MESH)
+
+    def cost_spread(side, d):
+        return pltpu.make_async_remote_copy(
+            src_ref=raw.at[2 - side, piece_of], dst_ref=raw.at[2 - side, piece_of], send_sem=cost_send.at[side, d],
+            recv_sem=cost_recv.at[side, d], device_id={"org": lax.rem(org + d, m)}, device_id_type=MESH)
 
     def source(side, j, h, start, count):
         row = jnp.where(side == 0, j - 1, rows - j)
         return warm.at[row, pl.ds(start, count), pl.ds(h * LANES, LANES)]
 
     def target(side, j, h, start, count):
-        if isinstance(j, int) and j == HALO:
-            return tail.at[1 - side, pl.ds(start, count), :]
+        if isinstance(j, int) and j >= STEPS:
+            return tail.at[1 - side, halves if j == HALO else h, pl.ds(start, count), :]
         row = jnp.where(side == 0, last + j, first - j)
         return grid.at[0, h, row, pl.ds(PAD + start, count), :]
 
@@ -129,9 +137,10 @@
         def body(j, carry):
             for h in range(halves):
                 for side in range(2):
-                    each_send(j, h, side, act)
+                    each_send(j, h if side else halves - 1 - h, side, act)
             return carry
-        lax.fori_loop(1, STEPS + 1, body, 0)
+        lax.fori_loop(1, STEPS, body, 0)
+        body(STEPS, 0)
         for side in range(2):
             each_send(HALO, 1 - side, side, act)
 
@@ -154,14 +163,14 @@
                         send_sem=row_send.at[side, unit(j, h), part], recv_sem=row_recv.at[side, unit(j, h), part],
                         device_id={"blk": bottom}, device_id_type=MESH).wait_recv()
 
-    def forward(j, h):
+    def forward(j):
         if relayed:
             for side in range(2):
                 @pl.when(me == via[side])
                 def _():
-                    k = 1 - side if h is None else h
-                    to_relay(side, j, k).wait_recv()
-                    from_relay(side, j, k).start()
+                    for h in (1 - side, side)[:1 if isinstance(j, int) and j == HALO else 2]:
+                        to_relay(side, j, h).wait_recv()
+                        from_relay(side, j, h).start()
 
     for side in range(2):
         @pl.when(sides[side][0])
@@ -192,16 +201,16 @@
     def fill_row(r):
         for h in range(halves):
             grid[0, h, r, inner, :] = jnp.full((cols, LANES), far_value, jnp.float32)
-    fill_row(0)
-    fill_row(total - 1)
-    for missing, block, begin in ((me == 0, 1, 1), (me == n - 1, 2, last + 1)):
+    for r in (0, 1, total - 2, total - 1):
+        fill_row(r)
+    for missing, block, begin in ((me == 0, 1, 2), (me == n - 1, 2, last + 1)):
         @pl.when(missing)
         def _():
             raw[block] = jnp.full(raw.shape[1:], far_value, jnp.float32)
             def fill(r, carry):
                 fill_row(begin + r)
                 return carry
-            lax.fori_loop(0, STEPS, fill, 0)
+            lax.fori_loop(0, STEPS - 1, fill, 0)
 
     def place(r):
         base = (me * rows + r - first) * cols
@@ -212,6 +221,13 @@
             for h in range(halves):
                 grid[0, h, r, at, :] = jnp.where(node == names[h], 0.0, grid[0, h, r, at, :])
 
+    for side in range(2):
+        @pl.when(sides[1 - side][0])
+        def _():
+            cost_copy(side).wait_recv()
+            for d in range(1, m):
+                cost_spread(side, d).start()
+
     for h in range(halves):
         own_rows(h).wait()
 
@@ -224,7 +240,8 @@
     for side in range(2):
         @pl.when(sides[1 - side][0])
         def _():
-            cost_copy(side).wait_recv()
+            for d in range(1, m):
+                cost_spread(side, d).wait_recv()
     turned[...] = jnp.transpose(raw[...].reshape(4 * 4 * rows, cols))
 
     def widen(i, carry):
@@ -299,8 +316,7 @@
         return jnp.where(q == 0, early, late)
 
     def opening(j, carry):
-        for h in both:
-            forward(j, h)
+        forward(j)
 
         def one(q, carry):
             stage(pair(q), j)
@@ -308,8 +324,7 @@
         return lax.fori_loop(0, 2, one, carry)
 
     def closing(j, carry):
-        for h in both:
-            forward(j, h)
+        forward(j)
 
         def one(q, carry):
             stage(pair(q), j)
@@ -372,7 +387,7 @@
             for i in range(cols // CHUNK):
                 at, mine = pl.ds(PAD + i * CHUNK, CHUNK), pl.ds(i * CHUNK, CHUNK)
                 node = lax.broadcasted_iota(jnp.int32, (CHUNK, LANES), 0) + (base + i * CHUNK)
-                value = jnp.where(node == names, 0.0, tail[halo, mine, :])
+                value = jnp.where(node == names, 0.0, tail[halo, halves, mine, :])
                 for t in range(1, STEPS + 1):
                     value = value + wide[2 + halo, r0 + step * t - 1, mine, :]
                 power = jnp.minimum(value, grid[STEPS % 2, halo, r0 + step * STEPS, at, :]) * RATE
@@ -402,15 +417,54 @@
 
     lax.fori_loop(1, 3, opening, 0)
     lax.fori_loop(3, STEPS, closing, 0)
-    for h in both:
-        forward(STEPS, h)
-    forward(HALO, None)
+    forward(STEPS)
+    forward(HALO)
+
+    def ahead(halo):
+        def diagonal(s, carry):
+            relax(jnp.where(halo == 0, first - STEPS + s, last + STEPS - s), s, both)
+            return carry
+        lax.fori_loop(1, STEPS + 1, diagonal, 0)
+
+    def chain(halo, h):
+        there = jnp.where(halo == 0, has_top, has_bottom)
+        r0 = jnp.where(halo == 0, first - STEPS, last + STEPS)
+        step = jnp.where(halo == 0, 1, -1)
+        q = jnp.where(halo == 0, 0, rows - 1)
+        arrive(halo, STEPS, h)
+
+        @pl.when(there)
+        def _():
+            base = (me * rows + r0 - first) * cols
+            for i in range(cols // CHUNK):
+                at, mine = pl.ds(PAD + i * CHUNK, CHUNK), pl.ds(i * CHUNK, CHUNK)
+                node = lax.broadcasted_iota(jnp.int32, (CHUNK, LANES), 0) + (base + i * CHUNK)
+                value = jnp.where(node == anchors[h], 0.0, tail[halo, h, mine, :])
+                grid[0, h, r0, at, :] = value
+                for t in range(1, STEPS + 1):
+                    r = r0 + step * t
+                    value = jnp.minimum(grid[t % 2, h, r, at, :], value + wide[2 + halo, r - 1, mine, :])
+                    grid[t % 2, h, r, at, :] = value
+
+        def settle(h_static):
+            for i in range(cols // CHUNK):
+                at, mine = pl.ds(PAD + i * CHUNK, CHUNK), pl.ds(i * CHUNK, CHUNK)
+                value = grid[STEPS % 2, h_static, q + first, at, :]
+                final[q, mine, pl.ds(h_static * LANES, LANES)] = value
+                power = value * RATE
+                decay[h_static, q + 1, at, :] = jnp.exp2(-power)
+                growth[h_static, q + 1, mine, :] = demand[h_static] * jnp.exp2(power)
+        for k in both:
+            @pl.when(h == k)
+            def _():
+                settle(k)
 
     def closing_side(q, carry):
         halo = pair(q)
-        stage(halo, STEPS)
-        finish(halo, STEPS)
+        ahead(halo)
+        chain(halo, halo)
         outer(halo)
+        chain(halo, 1 - halo)
         low = jnp.where(q == 0, jnp.where(late == 0, first + 1, first), jnp.where(late == 0, first, last))
         high = jnp.where(q == 0, jnp.where(late == 0, last, last - 1), jnp.where(late == 0, first, last))
         lax.fori_loop(low, high + 1, along, 0)
@@ -460,6 +514,10 @@
             cost_copy(side).wait_send()
             for p in range(m):
                 near_copy(side, p).wait_send()
+        @pl.when(sides[1 - side][0])
+        def _():
+            for d in range(1, m):
+                cost_spread(side, d).wait_send()
     all_sends(lambda copy: copy.wait_send())
     if relayed:
         for side in range(2):
@@ -469,7 +527,8 @@
                     for h in both:
                         from_relay(side, j, h).wait_send()
                     return carry
-                lax.fori_loop(1, STEPS + 1, body, 0)
+                lax.fori_loop(1, STEPS, body, 0)
+                body(STEPS, 0)
                 from_relay(side, HALO, 1 - side).wait_send()
 
 
@@ -506,7 +565,7 @@
             pltpu.VMEM((cols, 16 * rows), jnp.float32),
             pltpu.VMEM((halves, rows + 2, cols + 2 * PAD, LANES), jnp.float32),
             pltpu.VMEM((halves, rows + 2, cols, LANES), jnp.float32),
-            pltpu.VMEM((2, cols, LANES), jnp.float32),
+            pltpu.VMEM((2, halves + 1, cols, LANES), jnp.float32),
             pltpu.VMEM((units, cols - cols // 2, LANES), jnp.float32),
             pltpu.VMEM((4, rows, cols), jnp.float32),
             pltpu.VMEM((m, 4, rows, width), jnp.float32),
@@ -517,8 +576,8 @@
             dma((2, units, 2)),
             dma((units,)),
             dma((units,)),
-            dma((2,)),
-            dma((2,)),
+            dma((2, m)),
+            dma((2, m)),
             dma((max(m - 1, 1),)),
             dma((max(m - 1, 1),)),
             dma((2, m)),

time: 73.3 us -> 73.8 us (level)
  no operation moved by 1% of the time
where the time goes in v2:
time: 73.8 us; the launch traced here: 73.3 us
  Pallas kernels  72.7 us (99%)
    pallas_call x1, Pallas kernels, local(): pl.pallas_call(functools.partial(kernel, n, m, rows, cols, halves), out_s...  70.6 us
    pallas_call x1, Pallas kernels, local(): pl.pallas_call(functools.partial(leave, rows), out_shape=(jax.ShapeDtypeS...  2.08 us

profile of v2, /device:TPU:1, one launch (start us, length us, event | category | flops | bytes accessed | tf_op | source)
XLA Modules:
  0.0 73.3 jit_solution(2386811731101990339)
XLA Ops:
  0.6 70.6 %shard_map.59 = (f32[8,512,256]{2,1,0:T(8,128)S(1)}, f32[4,8,128]{2,1,0:T(8,128)S(1)}) custom-call(f32[8,512,256]{2,1,0:T(8,128)} %warm.1, f32[4,8,512]{2,1,0:T(8,128)} %costs.1, s32[2,1,128]{2,1,0:T(1,128)} %bitcast.2, f32[2,1,128]{2,1,0:T(1,128)} %bitcast.3), custom_call_target="tpu_custom_call" | custom-call | tf_op jit(solution)/shard_map/pallas_call | solution.py:553
  71.3 2.1 %shard_map.60 = (f32[8,512,256]{2,1,0:T(8,128)}, f32[4,8,128]{2,1,0:T(8,128)}) custom-call(f32[8,512,256]{2,1,0:T(8,128)S(1)} %get-tuple-element.4.labels, f32[4,8,128]{2,1,0:T(8,128)S(1)} %get-tuple-element.5.weights), custom_call_target="tpu_custom_call" | custom-call | tf_op jit(solution)/shard_map/pallas_call | solution.py:591

commit v3 on v2

--- a/solution.py
+++ b/solution.py
@@ -323,14 +323,9 @@
             return carry
         return lax.fori_loop(0, 2, one, carry)
 
-    def closing(j, carry):
-        forward(j)
-
-        def one(q, carry):
-            stage(pair(q), j)
-            finish(pair(q), j)
-            return carry
-        return lax.fori_loop(0, 2, one, carry)
+    def closing(halo, j):
+        stage(halo, j)
+        finish(halo, j)
 
     ones = jnp.ones((8, 2 * LANES), jnp.bfloat16)
 
@@ -414,11 +409,6 @@
         pltpu.make_async_remote_copy(
             src_ref=near_out.at[halo, p], dst_ref=near_in.at[halo, p], send_sem=near_send.at[halo, p],
             recv_sem=near_recv.at[halo, p], device_id={"blk": sides[halo][1], "org": p}, device_id_type=MESH).wait_recv()
-
-    lax.fori_loop(1, 3, opening, 0)
-    lax.fori_loop(3, STEPS, closing, 0)
-    forward(STEPS)
-    forward(HALO)
 
     def ahead(halo):
         def diagonal(s, carry):
@@ -459,20 +449,53 @@
             def _():
                 settle(k)
 
+    bulk = STEPS // 2
+
     def closing_side(q, carry):
         halo = pair(q)
+
+        def near(j, carry):
+            @pl.when(q == 0)
+            def _():
+                forward(j)
+            closing(halo, j)
+
+            @pl.when(q == 1)
+            def _():
+                edge_links(j)
+            return carry
+        lax.fori_loop(bulk + 1, STEPS, near, 0)
+
+        @pl.when(q == 0)
+        def _():
+            forward(STEPS)
+            forward(HALO)
         ahead(halo)
         chain(halo, halo)
         outer(halo)
         chain(halo, 1 - halo)
-        low = jnp.where(q == 0, jnp.where(late == 0, first + 1, first), jnp.where(late == 0, first, last))
-        high = jnp.where(q == 0, jnp.where(late == 0, last, last - 1), jnp.where(late == 0, first, last))
-        lax.fori_loop(low, high + 1, along, 0)
-        low = jnp.where(q == 0, jnp.where(late == 0, first + 1, first), jnp.where(late == 0, first, last - 1))
-        high = jnp.where(q == 0, jnp.where(late == 0, last - 1, last - 2), jnp.where(late == 0, first, last - 1))
-        lax.fori_loop(low, high + 1, across, 0)
+
+        @pl.when(q == 0)
+        def _():
+            low = jnp.where(late == 0, first + bulk, first)
+            lax.fori_loop(low, low + rows - bulk, along, 0)
+            lax.fori_loop(low, low + rows - bulk - 1, across, 0)
+
+        @pl.when(q == 1)
+        def _():
+            edge_links(STEPS)
         cross(halo)
         return carry
+
+    def edge_links(j):
+        r = jnp.where(late == 0, first - j + STEPS, last + j - STEPS)
+        along(r, 0)
+        across(r - late, 0)
+
+    lax.fori_loop(1, bulk, opening, 0)
+    forward(bulk)
+    for q in range(2):
+        closing(pair(q), bulk)
     lax.fori_loop(0, 2, closing_side, 0)
 
     ours = sums[...] * jnp.exp(-temper * raw[0]) * scale

time: 73.8 us -> 70.7 us (0.958)
  Pallas kernels: 72.7 us -> 69.9 us
    pallas_call x1, Pallas kernels: 70.6 us -> 67.9 us  [local(): pl.pallas_call(functools.partial(kernel, n, m, rows, cols, halves), out_s...]
where the time goes in v3:
time: 70.7 us; the launch traced here: 70.6 us
  Pallas kernels  69.9 us (99%)
    pallas_call x1, Pallas kernels, local(): pl.pallas_call(functools.partial(kernel, n, m, rows, cols, halves), out_s...  67.9 us
    pallas_call x1, Pallas kernels, local(): pl.pallas_call(functools.partial(leave, rows), out_shape=(jax.ShapeDtypeS...  2.08 us

profile of v3, /device:TPU:1, one launch (start us, length us, event | category | flops | bytes accessed | tf_op | source)
XLA Modules:
  0.0 70.6 jit_solution(4947478866531834936)
XLA Ops:
  0.6 67.9 %shard_map.59 = (f32[8,512,256]{2,1,0:T(8,128)S(1)}, f32[4,8,128]{2,1,0:T(8,128)S(1)}) custom-call(f32[8,512,256]{2,1,0:T(8,128)} %warm.1, f32[4,8,512]{2,1,0:T(8,128)} %costs.1, s32[2,1,128]{2,1,0:T(1,128)} %bitcast.2, f32[2,1,128]{2,1,0:T(1,128)} %bitcast.3), custom_call_target="tpu_custom_call" | custom-call | tf_op jit(solution)/shard_map/pallas_call | solution.py:576
  68.5 2.1 %shard_map.60 = (f32[8,512,256]{2,1,0:T(8,128)}, f32[4,8,128]{2,1,0:T(8,128)}) custom-call(f32[8,512,256]{2,1,0:T(8,128)S(1)} %get-tuple-element.4.labels, f32[4,8,128]{2,1,0:T(8,128)S(1)} %get-tuple-element.5.weights), custom_call_target="tpu_custom_call" | custom-call | tf_op jit(solution)/shard_map/pallas_call | solution.py:614

commit v4 on v3

--- a/solution.py
+++ b/solution.py
@@ -26,7 +26,7 @@
 
 def kernel(n, m, rows, cols, halves, warm, costs, anchors, demand, final, weights, grid, wide, raw, turned, decay, growth, tail,
            relay, sums, share, landed, near_out, near_in, row_send, row_recv, relay_in, relay_out, cost_send, cost_recv,
-           org_send, org_recv, near_send, near_recv, local_sem):
+           org_send, org_recv, near_send, near_recv, lend, lend_in, lend_out, lend_recv, ready, local_sem):
     me = lax.axis_index("blk")
     org = lax.axis_index("org")
     has_top = me > 0
@@ -47,15 +47,25 @@
     late = lax.rem(me, 2)
     early = 1 - late
     last_unit = STEPS * halves
+    plans = ((m - 1, 0, cols * 5 // 8), (m - 2, 1, cols * 3 // 16)) if relayed and m == 4 else ()
+    paired = (me != 0) & (me != n - 1) & (me != mid - 1) & (me != mid)
 
     barrier = pltpu.get_barrier_semaphore()
     for there, who in sides:
         @pl.when(there)
         def _():
-            for p in range(m):
-                pl.semaphore_signal(barrier, inc=1, device_id={"blk": who, "org": p}, device_id_type=MESH)
-    for d in range(1, m):
-        pl.semaphore_signal(barrier, inc=1, device_id={"org": lax.rem(org + d, m)}, device_id_type=MESH)
+            pl.semaphore_signal(barrier, inc=1, device_id={"blk": who}, device_id_type=MESH)
+
+    def greet(signal, p):
+        pl.semaphore_signal(signal, inc=1, device_id={"org": p}, device_id_type=MESH)
+        for there, who in sides:
+            @pl.when(there)
+            def _():
+                pl.semaphore_signal(signal, inc=1, device_id={"blk": who, "org": p}, device_id_type=MESH)
+    for p in range(1, m):
+        @pl.when(org < p)
+        def _():
+            greet(barrier, p)
     if relayed:
         for a, b in ((mid - 1, 0), (mid - 1, n - 1), (mid, 0), (mid, n - 1)):
             for mine, other in ((a, b), (b, a)):
@@ -72,7 +82,8 @@
             local_sem.at[h])
     for h in range(halves):
         own_rows(h).start()
-    pl.semaphore_wait(barrier, m - 1 + jnp.where(has_top, m, 0) + jnp.where(has_bottom, m, 0)
+    around = jnp.where(has_top, 1, 0) + jnp.where(has_bottom, 1, 0)
+    pl.semaphore_wait(barrier, around + org * (1 + around)
                       + (jnp.where((me == 0) | (me == n - 1) | (me == mid) | (me == mid - 1), 2, 0) if relayed else 0))
 
     part = 4 // m
@@ -132,6 +143,40 @@
             def _():
                 act(to_relay(side, j, h))
                 act(row_copy(side, j, h, cut))
+
+    def lend_copy(side, via_plane, moved):
+        kept = cols - moved
+        return pltpu.make_async_remote_copy(
+            src_ref=source(side, HALO, 1 - side, kept, moved), dst_ref=lend.at[pl.ds(0, moved)],
+            send_sem=row_send.at[side, last_unit, 1], recv_sem=lend_in.at[0],
+            device_id={"blk": sides[side][1], "org": via_plane}, device_id_type=MESH)
+
+    def lend_on(from_plane, moved):
+        return pltpu.make_async_remote_copy(
+            src_ref=lend.at[pl.ds(0, moved)], dst_ref=tail.at[late, halves, pl.ds(cols - moved, moved), :],
+            send_sem=lend_out.at[0], recv_sem=lend_recv.at[0], device_id={"org": from_plane}, device_id_type=MESH)
+
+    def outer_send(side, act):
+        there, split = sides[side][0], splits[side]
+        lending = paired & (late == side)
+        plain = there
+        for from_plane, via_plane, moved in plans:
+            here = lending & (org == from_plane)
+            plain = plain & jnp.logical_not(here)
+
+            @pl.when(here)
+            def _():
+                act(row_copy(side, HALO, 1 - side, cols - moved))
+                act(lend_copy(side, via_plane, moved))
+
+        @pl.when(plain & jnp.logical_not(split) if relayed else plain)
+        def _():
+            act(row_copy(side, HALO, 1 - side, cols))
+        if relayed:
+            @pl.when(split)
+            def _():
+                act(to_relay(side, HALO, 1 - side))
+                act(row_copy(side, HALO, 1 - side, cut))
 
     def all_sends(act):
         def body(j, carry):
@@ -142,7 +187,7 @@
         lax.fori_loop(1, STEPS, body, 0)
         body(STEPS, 0)
         for side in range(2):
-            each_send(HALO, 1 - side, side, act)
+            outer_send(side, act)
 
     def arrive(halo, j, h):
         side = 1 - halo
@@ -162,6 +207,25 @@
                         src_ref=source(0, 1, 0, start, count), dst_ref=target(side, j, h, start, count),
                         send_sem=row_send.at[side, unit(j, h), part], recv_sem=row_recv.at[side, unit(j, h), part],
                         device_id={"blk": bottom}, device_id_type=MESH).wait_recv()
+
+    def arrive_outer(halo):
+        lending = paired & (late == halo)
+        plain = jnp.bool_(True)
+        for from_plane, _, moved in plans:
+            here = lending & (org == from_plane)
+            plain = plain & jnp.logical_not(here)
+
+            @pl.when(here)
+            def _():
+                pltpu.make_async_remote_copy(
+                    src_ref=source(0, 1, 0, 0, cols - moved), dst_ref=target(1 - halo, HALO, halo, 0, cols - moved),
+                    send_sem=row_send.at[1 - halo, last_unit, 0], recv_sem=row_recv.at[1 - halo, last_unit, 0],
+                    device_id={"blk": bottom}, device_id_type=MESH).wait_recv()
+                lend_on(from_plane, moved).wait_recv()
+
+        @pl.when(plain)
+        def _():
+            arrive(halo, HALO, halo)
 
     def forward(j):
         if relayed:
@@ -177,6 +241,10 @@
         def _():
             cost_copy(side).start()
     all_sends(lambda copy: copy.start())
+    for p in range(m - 1):
+        @pl.when(org > p)
+        def _():
+            greet(ready, p)
 
     edge = jnp.full((PAD, LANES), far_value, jnp.float32)
     zero_edge = jnp.zeros((PAD, LANES), jnp.float32)
@@ -221,6 +289,9 @@
             for h in range(halves):
                 grid[0, h, r, at, :] = jnp.where(node == names[h], 0.0, grid[0, h, r, at, :])
 
+    @pl.when(org < m - 1)
+    def _():
+        pl.semaphore_wait(ready, (m - 1 - org) * (1 + around))
     for side in range(2):
         @pl.when(sides[1 - side][0])
         def _():
@@ -373,7 +444,7 @@
         step = jnp.where(halo == 0, 1, -1)
         own = jnp.where(halo == 0, 1, rows)
         other = jnp.where(halo == 0, 0, rows + 1)
-        arrive(halo, HALO, halo)
+        arrive_outer(halo)
 
         @pl.when(there)
         def _():
@@ -493,6 +564,13 @@
         across(r - late, 0)
 
     lax.fori_loop(1, bulk, opening, 0)
+    for from_plane, via_plane, moved in plans:
+        @pl.when(paired & (org == via_plane))
+        def _():
+            pltpu.make_async_remote_copy(
+                src_ref=lend.at[pl.ds(0, moved)], dst_ref=lend.at[pl.ds(0, moved)], send_sem=lend_out.at[0],
+                recv_sem=lend_in.at[0], device_id={"org": from_plane}, device_id_type=MESH).wait_recv()
+            lend_on(from_plane, moved).start()
     forward(bulk)
     for q in range(2):
         closing(pair(q), bulk)
@@ -542,6 +620,10 @@
             for d in range(1, m):
                 cost_spread(side, d).wait_send()
     all_sends(lambda copy: copy.wait_send())
+    for from_plane, via_plane, moved in plans:
+        @pl.when(paired & (org == via_plane))
+        def _():
+            lend_on(from_plane, moved).wait_send()
     if relayed:
         for side in range(2):
             @pl.when(me == via[side])
@@ -605,6 +687,11 @@
             dma((max(m - 1, 1),)),
             dma((2, m)),
             dma((2, m)),
+            pltpu.VMEM((cols * 5 // 8, LANES), jnp.float32),
+            dma((1,)),
+            dma((1,)),
+            dma((1,)),
+            pltpu.SemaphoreType.REGULAR,
             dma((halves + 1,)),
         ],
         compiler_params=pltpu.CompilerParams(collective_id=0, has_side_effects=True, vmem_limit_bytes=58 * 1024 * 1024),

time: 70.7 us -> 69.5 us (0.983)
  Pallas kernels: 69.9 us -> 68.7 us
    pallas_call x1, Pallas kernels: 67.9 us -> 66.6 us  [local(): pl.pallas_call(functools.partial(kernel, n, m, rows, cols, halves), out_s...]
where the time goes in v4:
time: 69.5 us; the launch traced here: 69.4 us
  Pallas kernels  68.7 us (99%)
    pallas_call x1, Pallas kernels, local(): pl.pallas_call(functools.partial(kernel, n, m, rows, cols, halves), out_s...  66.6 us
    pallas_call x1, Pallas kernels, local(): pl.pallas_call(functools.partial(leave, rows), out_shape=(jax.ShapeDtypeS...  2.08 us

profile of v4, /device:TPU:1, one launch (start us, length us, event | category | flops | bytes accessed | tf_op | source)
XLA Modules:
  0.0 69.4 jit_solution(9315579892904446399)
XLA Ops:
  0.6 66.6 %shard_map.59 = (f32[8,512,256]{2,1,0:T(8,128)S(1)}, f32[4,8,128]{2,1,0:T(8,128)S(1)}) custom-call(f32[8,512,256]{2,1,0:T(8,128)} %warm.1, f32[4,8,512]{2,1,0:T(8,128)} %costs.1, s32[2,1,128]{2,1,0:T(1,128)} %bitcast.2, f32[2,1,128]{2,1,0:T(1,128)} %bitcast.3), custom_call_target="tpu_custom_call" | custom-call | tf_op jit(solution)/shard_map/pallas_call | solution.py:658
  67.3 2.1 %shard_map.60 = (f32[8,512,256]{2,1,0:T(8,128)}, f32[4,8,128]{2,1,0:T(8,128)}) custom-call(f32[8,512,256]{2,1,0:T(8,128)S(1)} %get-tuple-element.4.labels, f32[4,8,128]{2,1,0:T(8,128)S(1)} %get-tuple-element.5.weights), custom_call_target="tpu_custom_call" | custom-call | tf_op jit(solution)/shard_map/pallas_call | solution.py:701

commit v5 on v4

--- a/solution.py
+++ b/solution.py
@@ -24,9 +24,9 @@
 MESH = pl.DeviceIdType.MESH
 
 
-def kernel(n, m, rows, cols, halves, warm, costs, anchors, demand, final, weights, grid, wide, raw, turned, decay, growth, tail,
+def kernel(n, m, rows, cols, halves, warm, costs, anchors_in, demand_in, final, weights, grid, wide, raw, turned, decay, growth, tail,
            relay, sums, share, landed, near_out, near_in, row_send, row_recv, relay_in, relay_out, cost_send, cost_recv,
-           org_send, org_recv, near_send, near_recv, lend, lend_in, lend_out, lend_recv, ready, local_sem):
+           org_send, org_recv, near_send, near_recv, lend, lend_in, lend_out, lend_recv, ready, anchors, demand, fees, local_sem):
     me = lax.axis_index("blk")
     org = lax.axis_index("org")
     has_top = me > 0
@@ -47,7 +47,7 @@
     late = lax.rem(me, 2)
     early = 1 - late
     last_unit = STEPS * halves
-    plans = ((m - 1, 0, cols * 5 // 8), (m - 2, 1, cols * 3 // 16)) if relayed and m == 4 else ()
+    plans = ((m - 1, 0, cols * 13 // 16), (m - 2, 1, cols * 9 // 32)) if relayed and m == 4 else ()
     paired = (me != 0) & (me != n - 1) & (me != mid - 1) & (me != mid)
 
     barrier = pltpu.get_barrier_semaphore()
@@ -74,6 +74,10 @@
                     pl.semaphore_signal(barrier, inc=1, device_id={"blk": other}, device_id_type=MESH)
     own_cost = pltpu.make_async_copy(costs, raw.at[0], local_sem.at[halves])
     own_cost.start()
+    listed = (pltpu.make_async_copy(anchors_in, anchors, local_sem.at[halves + 1]),
+              pltpu.make_async_copy(demand_in, demand, local_sem.at[halves + 2]))
+    for copy in listed:
+        copy.start()
 
     def own_rows(h):
         return pltpu.make_async_copy(
@@ -299,6 +303,8 @@
             for d in range(1, m):
                 cost_spread(side, d).start()
 
+    for copy in listed:
+        copy.wait()
     for h in range(halves):
         own_rows(h).wait()
 
@@ -465,8 +471,7 @@
             link(own, other, 0, (halo,), mine_store)
 
             def near_store(at, part):
-                fee = raw[1 + halo, 3 - halo, pl.ds(jnp.where(halo == 0, rows - 1, 0), 1), at]
-                value = part * jnp.exp(-temper * fee) * scale
+                value = part * fees[4 + halo, pl.ds(jnp.where(halo == 0, rows - 1, 0), 1), at]
                 for c in range(0, at.size, width):
                     near_out[halo, (at.start + c) // width] = value[:, c:c + width]
             link(other, own, 0, (halo,), near_store)
@@ -563,6 +568,11 @@
         along(r, 0)
         across(r - late, 0)
 
+    for k in range(4):
+        fees[k] = jnp.exp(-temper * raw[0, k]) * scale
+    for halo in range(2):
+        fees[4 + halo] = jnp.exp(-temper * raw[1 + halo, 3 - halo]) * scale
+
     lax.fori_loop(1, bulk, opening, 0)
     for from_plane, via_plane, moved in plans:
         @pl.when(paired & (org == via_plane))
@@ -576,22 +586,52 @@
         closing(pair(q), bulk)
     lax.fori_loop(0, 2, closing_side, 0)
 
-    ours = sums[...] * jnp.exp(-temper * raw[0]) * scale
+    for halo in range(2):
+        @pl.when(sides[halo][0])
+        def _():
+            for p in range(m):
+                near_copy(halo, p).start()
     for p in range(m):
-        share[p] = ours[:, :, p * width:(p + 1) * width]
+        share[p] = sums[:, :, p * width:(p + 1) * width] * fees[0:4, :, p * width:(p + 1) * width]
 
     def org_copy(d):
         peer = lax.rem(org + d, m)
         return pltpu.make_async_remote_copy(
             src_ref=share.at[peer], dst_ref=landed.at[d - 1], send_sem=org_send.at[d - 1], recv_sem=org_recv.at[d - 1],
             device_id={"org": peer}, device_id_type=MESH)
-    for halo in range(2):
-        @pl.when(sides[halo][0])
-        def _():
-            for p in range(m):
-                near_copy(halo, p).start()
     for d in range(1, m):
         org_copy(d).start()
+    for side in range(2):
+        @pl.when(sides[side][0])
+        def _():
+            cost_copy(side).wait_send()
+        @pl.when(sides[1 - side][0])
+        def _():
+            for d in range(1, m):
+                cost_spread(side, d).wait_send()
+    all_sends(lambda copy: copy.wait_send())
+    for from_plane, via_plane, moved in plans:
+        @pl.when(paired & (org == via_plane))
+        def _():
+            lend_on(from_plane, moved).wait_send()
+    if relayed:
+        for side in range(2):
+            @pl.when(me == via[side])
+            def _():
+                def body(j, carry):
+                    for h in both:
+                        from_relay(side, j, h).wait_send()
+                    return carry
+                lax.fori_loop(1, STEPS, body, 0)
+                body(STEPS, 0)
+                from_relay(side, HALO, 1 - side).wait_send()
+    for d in range(1, m):
+        org_copy(d).wait_send()
+    for side in range(2):
+        @pl.when(sides[side][0])
+        def _():
+            for p in range(m):
+                near_copy(side, p).wait_send()
     result = share[org]
     for d in range(1, m):
         org_copy(d).wait_recv()
@@ -606,35 +646,6 @@
                 near_wait(halo, p)
                 extra += near_in[halo, p]
             weights[2 + halo, pl.ds(at, 1), :] = extra
-
-    for d in range(1, m):
-        org_copy(d).wait_send()
-    for side in range(2):
-        @pl.when(sides[side][0])
-        def _():
-            cost_copy(side).wait_send()
-            for p in range(m):
-                near_copy(side, p).wait_send()
-        @pl.when(sides[1 - side][0])
-        def _():
-            for d in range(1, m):
-                cost_spread(side, d).wait_send()
-    all_sends(lambda copy: copy.wait_send())
-    for from_plane, via_plane, moved in plans:
-        @pl.when(paired & (org == via_plane))
-        def _():
-            lend_on(from_plane, moved).wait_send()
-    if relayed:
-        for side in range(2):
-            @pl.when(me == via[side])
-            def _():
-                def body(j, carry):
-                    for h in both:
-                        from_relay(side, j, h).wait_send()
-                    return carry
-                lax.fori_loop(1, STEPS, body, 0)
-                body(STEPS, 0)
-                from_relay(side, HALO, 1 - side).wait_send()
 
 
 def leave(rows, labels, weights, labels_out, weights_out, sems):
@@ -661,7 +672,7 @@
             pltpu.VMEM((rows, cols, count), jnp.float32),
             pltpu.VMEM((4, rows, width), jnp.float32),
         ),
-        in_specs=[any_space, any_space, vmem, vmem],
+        in_specs=[any_space] * 4,
         out_specs=(vmem, vmem),
         scratch_shapes=[
             pltpu.VMEM((2, halves, total, cols + 2 * PAD, LANES), jnp.float32),
@@ -687,12 +698,15 @@
             dma((max(m - 1, 1),)),
             dma((2, m)),
             dma((2, m)),
-            pltpu.VMEM((cols * 5 // 8, LANES), jnp.float32),
+            pltpu.VMEM((cols * 13 // 16, LANES), jnp.float32),
             dma((1,)),
             dma((1,)),
             dma((1,)),
             pltpu.SemaphoreType.REGULAR,
-            dma((halves + 1,)),
+            pltpu.VMEM((halves, 1, LANES), jnp.int32),
+            pltpu.VMEM((halves, 1, LANES), jnp.float32),
+            pltpu.VMEM((6, rows, cols), jnp.float32),
+            dma((halves + 3,)),
         ],
         compiler_params=pltpu.CompilerParams(collective_id=0, has_side_effects=True, vmem_limit_bytes=58 * 1024 * 1024),
     )(warm_labels, link_costs, anchor_nodes.reshape(halves, 1, LANES), demand.reshape(halves, 1, LANES))

time: 69.5 us -> 69.1 us (level)
  no operation moved by 1% of the time
where the time goes in v5:
time: 69.1 us; the launch traced here: 69 us
  Pallas kernels  68.3 us (99%)
    pallas_call x1, Pallas kernels, local(): pl.pallas_call(functools.partial(kernel, n, m, rows, cols, halves), out_s...  66.3 us
    pallas_call x1, Pallas kernels, local(): pl.pallas_call(functools.partial(leave, rows), out_shape=(jax.ShapeDtypeS...  2.08 us

profile of v5, /device:TPU:1, one launch (start us, length us, event | category | flops | bytes accessed | tf_op | source)
XLA Modules:
  0.0 69.0 jit_solution(17298188340725225224)
XLA Ops:
  0.6 66.3 %shard_map.59 = (f32[8,512,256]{2,1,0:T(8,128)S(1)}, f32[4,8,128]{2,1,0:T(8,128)S(1)}) custom-call(f32[8,512,256]{2,1,0:T(8,128)} %warm.1, f32[4,8,512]{2,1,0:T(8,128)} %costs.1, s32[2,1,128]{2,1,0:T(1,128)} %bitcast.2, f32[2,1,128]{2,1,0:T(1,128)} %bitcast.3), custom_call_target="tpu_custom_call" | custom-call | tf_op jit(solution)/shard_map/pallas_call | solution.py:669
  66.9 2.1 %shard_map.60 = (f32[8,512,256]{2,1,0:T(8,128)}, f32[4,8,128]{2,1,0:T(8,128)}) custom-call(f32[8,512,256]{2,1,0:T(8,128)S(1)} %get-tuple-element.4.labels, f32[4,8,128]{2,1,0:T(8,128)S(1)} %get-tuple-element.5.weights), custom_call_target="tpu_custom_call" | custom-call | tf_op jit(solution)/shard_map/pallas_call | solution.py:715

commit v6 on v5

--- a/solution.py
+++ b/solution.py
@@ -189,9 +189,12 @@
                     each_send(j, h if side else halves - 1 - h, side, act)
             return carry
         lax.fori_loop(1, STEPS, body, 0)
-        body(STEPS, 0)
+        for side in range(2):
+            each_send(STEPS, 1 - side, side, act)
         for side in range(2):
             outer_send(side, act)
+        for side in range(2):
+            each_send(STEPS, side, side, act)
 
     def arrive(halo, j, h):
         side = 1 - halo
@@ -475,11 +478,14 @@
                 for c in range(0, at.size, width):
                     near_out[halo, (at.start + c) // width] = value[:, c:c + width]
             link(other, own, 0, (halo,), near_store)
+            for p in range(m):
+                near_copy(halo, p).start()
 
     def near_copy(halo, p):
         return pltpu.make_async_remote_copy(
             src_ref=near_out.at[halo, p], dst_ref=near_in.at[1 - halo, org], send_sem=near_send.at[halo, p],
-            recv_sem=near_recv.at[1 - halo, org], device_id={"blk": sides[halo][1], "org": p}, device_id_type=MESH)
+            recv_sem=near_recv.at[1 - halo, org],
+            device_id={"blk": jnp.where(halo == 0, top, bottom), "org": p}, device_id_type=MESH)
 
     def near_wait(halo, p):
         pltpu.make_async_remote_copy(
@@ -492,7 +498,7 @@
             return carry
         lax.fori_loop(1, STEPS + 1, diagonal, 0)
 
-    def chain(halo, h):
+    def chain(halo, h, kept):
         there = jnp.where(halo == 0, has_top, has_bottom)
         r0 = jnp.where(halo == 0, first - STEPS, last + STEPS)
         step = jnp.where(halo == 0, 1, -1)
@@ -506,11 +512,13 @@
                 at, mine = pl.ds(PAD + i * CHUNK, CHUNK), pl.ds(i * CHUNK, CHUNK)
                 node = lax.broadcasted_iota(jnp.int32, (CHUNK, LANES), 0) + (base + i * CHUNK)
                 value = jnp.where(node == anchors[h], 0.0, tail[halo, h, mine, :])
-                grid[0, h, r0, at, :] = value
+                if kept:
+                    grid[0, h, r0, at, :] = value
                 for t in range(1, STEPS + 1):
                     r = r0 + step * t
                     value = jnp.minimum(grid[t % 2, h, r, at, :], value + wide[2 + halo, r - 1, mine, :])
-                    grid[t % 2, h, r, at, :] = value
+                    if kept or t == STEPS:
+                        grid[t % 2, h, r, at, :] = value
 
         def settle(h_static):
             for i in range(cols // CHUNK):
@@ -547,9 +555,10 @@
             forward(STEPS)
             forward(HALO)
         ahead(halo)
-        chain(halo, halo)
+        chain(halo, halo, True)
         outer(halo)
-        chain(halo, 1 - halo)
+        cross(halo)
+        chain(halo, 1 - halo, False)
 
         @pl.when(q == 0)
         def _():
@@ -560,7 +569,6 @@
         @pl.when(q == 1)
         def _():
             edge_links(STEPS)
-        cross(halo)
         return carry
 
     def edge_links(j):
@@ -586,11 +594,6 @@
         closing(pair(q), bulk)
     lax.fori_loop(0, 2, closing_side, 0)
 
-    for halo in range(2):
-        @pl.when(sides[halo][0])
-        def _():
-            for p in range(m):
-                near_copy(halo, p).start()
     for p in range(m):
         share[p] = sums[:, :, p * width:(p + 1) * width] * fees[0:4, :, p * width:(p + 1) * width]
 

time: 69.1 us -> 68.3 us (0.988)
  Pallas kernels: 68.3 us -> 67.4 us
    pallas_call x1, Pallas kernels: 66.3 us -> 65.3 us  [local(): pl.pallas_call(functools.partial(kernel, n, m, rows, cols, halves), out_s...]
where the time goes in v6:
time: 68.3 us; the launch traced here: 68 us
  Pallas kernels  67.4 us (99%)
    pallas_call x1, Pallas kernels, local(): pl.pallas_call(functools.partial(kernel, n, m, rows, cols, halves), out_s...  65.3 us
    pallas_call x1, Pallas kernels, local(): pl.pallas_call(functools.partial(leave, rows), out_shape=(jax.ShapeDtypeS...  2.08 us

profile of v6, /device:TPU:1, one launch (start us, length us, event | category | flops | bytes accessed | tf_op | source)
XLA Modules:
  0.0 68.0 jit_solution(5452924932739026545)
XLA Ops:
  0.6 65.3 %shard_map.59 = (f32[8,512,256]{2,1,0:T(8,128)S(1)}, f32[4,8,128]{2,1,0:T(8,128)S(1)}) custom-call(f32[8,512,256]{2,1,0:T(8,128)} %warm.1, f32[4,8,512]{2,1,0:T(8,128)} %costs.1, s32[2,1,128]{2,1,0:T(1,128)} %bitcast.2, f32[2,1,128]{2,1,0:T(1,128)} %bitcast.3), custom_call_target="tpu_custom_call" | custom-call | tf_op jit(solution)/shard_map/pallas_call | solution.py:672
  66.0 2.1 %shard_map.60 = (f32[8,512,256]{2,1,0:T(8,128)}, f32[4,8,128]{2,1,0:T(8,128)}) custom-call(f32[8,512,256]{2,1,0:T(8,128)S(1)} %get-tuple-element.4.labels, f32[4,8,128]{2,1,0:T(8,128)S(1)} %get-tuple-element.5.weights), custom_call_target="tpu_custom_call" | custom-call | tf_op jit(solution)/shard_map/pallas_call | solution.py:718

commit v7 on v6

--- a/solution.py
+++ b/solution.py
@@ -652,8 +652,7 @@
 
 
 def leave(rows, labels, weights, labels_out, weights_out, sems):
-    copies = [pltpu.make_async_copy(labels.at[r], labels_out.at[r], sems.at[r]) for r in range(rows)]
-    copies.append(pltpu.make_async_copy(weights, weights_out, sems.at[rows]))
+    copies = [pltpu.make_async_copy(labels, labels_out, sems.at[0]), pltpu.make_async_copy(weights, weights_out, sems.at[1])]
     for copy in copies:
         copy.start()
     for copy in copies:
@@ -723,7 +722,7 @@
         ),
         in_specs=[vmem, vmem],
         out_specs=(any_space, any_space),
-        scratch_shapes=[dma((rows + 1,))],
+        scratch_shapes=[dma((2,))],
         compiler_params=pltpu.CompilerParams(vmem_limit_bytes=8 * 1024 * 1024),
     )(labels, weights)
 

time: 68.3 us -> 68.2 us (level)
  no operation moved by 1% of the time
where the time goes in v7:
time: 68.2 us; the launch traced here: 68 us
  Pallas kernels  67.3 us (99%)
    pallas_call x1, Pallas kernels, local(): pl.pallas_call(functools.partial(kernel, n, m, rows, cols, halves), out_s...  65.3 us
    pallas_call x1, Pallas kernels, local(): pl.pallas_call(functools.partial(leave, rows), out_shape=(jax.ShapeDtypeS...  2.03 us

profile of v7, /device:TPU:1, one launch (start us, length us, event | category | flops | bytes accessed | tf_op | source)
XLA Modules:
  0.0 68.0 jit_solution(11741560834249567590)
XLA Ops:
  0.6 65.3 %shard_map.59 = (f32[8,512,256]{2,1,0:T(8,128)S(1)}, f32[4,8,128]{2,1,0:T(8,128)S(1)}) custom-call(f32[8,512,256]{2,1,0:T(8,128)} %warm.1, f32[4,8,512]{2,1,0:T(8,128)} %costs.1, s32[2,1,128]{2,1,0:T(1,128)} %bitcast.2, f32[2,1,128]{2,1,0:T(1,128)} %bitcast.3), custom_call_target="tpu_custom_call" | custom-call | tf_op jit(solution)/shard_map/pallas_call | solution.py:671
  66.0 2.0 %shard_map.60 = (f32[8,512,256]{2,1,0:T(8,128)}, f32[4,8,128]{2,1,0:T(8,128)}) custom-call(f32[8,512,256]{2,1,0:T(8,128)S(1)} %get-tuple-element.4.labels, f32[4,8,128]{2,1,0:T(8,128)S(1)} %get-tuple-element.5.weights), custom_call_target="tpu_custom_call" | custom-call | tf_op jit(solution)/shard_map/pallas_call | solution.py:717
